TPU v7x, 256 devices: a whole 4x4x8 slice. The times are simulated.
256 devices in a mesh: dp: 16 (over y, x_lo, core), mp: 16 (over x_hi, z).
Axes of the slice: x: 4 (x_hi: 2, x_lo: 2; x = x_hi * 2 + x_lo), y: 4, z: 8, core: 2. Of those that a mesh axis runs over, the one named last changes fastest.
Arguments:
- token_ids: int32 [32, 16], replicated, may hold values from 0 to 64511
- prompt_lengths: int32 [32], replicated, may hold values from 128 to 6144, as said below
- cache_codes: bfloat16 [32, 6144, 2, 1024], P('dp', 'mp'), may hold values from -1 to 1
- cache_scales: bfloat16 [32, 48, 2, 1024], P('dp', 'mp'), may hold values from 0.03 to 400
- embedding: bfloat16 [64512, 8192], P('mp', 'dp'), may hold values from -12 to 12
- norm_gain: bfloat16 [8192], P('dp'), may hold values from 0.099609375 to 1.8984375
- query_weight: bfloat16 [8192, 8192], P('dp', 'mp'), may hold values from -0.0625 to 0.0625
- key_value_weight: bfloat16 [8192, 2, 1024], P('dp'), may hold values from -0.0625 to 0.0625
- output_weight: bfloat16 [8192, 8192], P('mp', 'dp'), may hold values from -0.0625 to 0.0625
Outputs:
- layer_out: bfloat16 [32, 16, 8192], P(None, None, 'dp')
Inputs may be any that keep to these rules, and one draw needn't show every extreme that they name: `prompt_lengths`: each a multiple of 128; some row has exactly 6144 in every draw.
All inputs are finite; a program needn't handle non-finite values.
Results may differ from a plain program's by a relative error of at most 0.0065.
The roundings to bfloat16 on the way count: a program that leaves them out, or rounds other values in their place, can miss the bound.
Values may be sent and summed in bfloat16 or wider, within the bound.
A program may use at most 128 MiB of HBM per device.

v0:
```python
import math
import jax
import jax.numpy as jnp
from jax import lax
from jax.sharding import PartitionSpec as P

D = 8192
QH = 64
KVH = 8
HEAD = 128
FACTOR_GROUP = 128
NEW = 16
ROPE_BASE = 500000.0
EPSILON = 1e-05
LOWEST = -1e30


def split_up(shard, dim, devices):
    before, after = (shard.shape[:dim], shard.shape[dim + 1 :])
    return jnp.moveaxis(shard.reshape(*before, devices, -1, *after), dim, 0)


def sent_and_summed(shard, axis, dim):
    pieces = split_up(shard, dim, lax.axis_size(axis))
    arrived = lax.all_to_all(pieces, axis, split_axis=0, concat_axis=0, tiled=True)
    return arrived.sum(axis=0)


def rows_for(lines, devices):
    spare = -len(lines) % devices
    return jnp.pad(lines, [(0, spare)] + [(0, 0)] * (lines.ndim - 1))


def joined_along(pieces, dim):
    shape = list(pieces.shape[1:])
    shape[dim] *= pieces.shape[0]
    return jnp.moveaxis(pieces, 0, dim).reshape(shape)


def copy_for_each(shard, axis):
    copies = jnp.broadcast_to(shard, (lax.axis_size(axis), *shard.shape))
    return lax.all_to_all(copies, axis, split_axis=0, concat_axis=0, tiled=True)


def gather_directly(shard, axis, dim):
    return joined_along(copy_for_each(shard, axis), dim)


def total_of(shard, axes):
    lines = shard.reshape(-1, shard.shape[-1])
    own = sent_and_summed(rows_for(lines, lax.axis_size(axes)), axes, 0)
    whole = gather_directly(own, axes, 0)
    return whole[: len(lines)].reshape(shard.shape)


def sent_together(arrays, axis, dim, along):
    ends, at = ([], 0)
    for a in arrays[:-1]:
        at += a.shape[along]
        ends.append(at)
    both = jnp.concatenate(arrays, axis=along)
    return tuple(jnp.split(lax.all_gather(both, axis, axis=dim, tiled=True), ends, axis=along))


def collected_together(shard, axis):
    leaves = jax.tree.leaves(shard)
    order = sorted(range(len(leaves)), key=lambda k: -leaves[k].size)
    width = (1, *leaves[order[0]].shape)[-1]
    lines = [
        jnp.pad(leaves[k].reshape(-1), (0, -leaves[k].size % width)).reshape(-1, width)
        for k in order
    ]
    both, at, found = (copy_for_each(jnp.concatenate(lines), axis), 0, {})
    for k, line in zip(order, lines):
        share = both[:, at : at + len(line)].reshape(len(both), -1)
        found[k] = share[:, : leaves[k].size].reshape(-1, *leaves[k].shape)
        at += len(line)
    numbers = iter(range(len(leaves)))
    return jax.tree.map(lambda _: found[next(numbers)], shard)


def combined_pairwise(pieces, combine):
    while len(jax.tree.leaves(pieces)[0]) > 1:
        pieces = jax.vmap(combine)(
            *(jax.tree.map(lambda part: part[side::2], pieces) for side in (0, 1))
        )
    return jax.tree.map(lambda part: part[0], pieces)


def joined_all(shard, axis, combine):
    pieces = collected_together(shard, axis)
    return combined_pairwise(pieces, combine)


def sent_together_2(arrays, axis, dim, along):
    widths = [math.prod(a.shape[along:]) for a in arrays]
    both = jnp.concatenate(
        [a.reshape(*a.shape[:along], w) for a, w in zip(arrays, widths)], axis=along
    )
    whole = lax.psum_scatter(both, axis, scatter_dimension=dim, tiled=True)
    pieces = jnp.split(whole, [sum(widths[:k]) for k in range(1, len(widths))], axis=along)
    return tuple(
        (b.reshape(*whole.shape[:along], *a.shape[along:]) for a, b in zip(arrays, pieces))
    )


def rotate(values, positions):
    width = values.shape[-1]
    half_width = width // 2
    exponent = jnp.arange(half_width, dtype=jnp.float32) * (2.0 / width)
    rates = jnp.exp(-jnp.log(ROPE_BASE) * exponent)
    angles = positions[..., None].astype(jnp.float32) * rates
    cosine = jnp.cos(angles)
    sinus_term = jnp.sin(angles)
    first = values[..., :half_width]
    second = values[..., half_width:]
    return jnp.concatenate(
        [first * cosine - second * sinus_term, second * cosine + first * sinus_term], axis=-1
    )


def tensor_total(partial_value):
    return total_of(partial_value, "mp")


def combine_totals(earlier, later):
    largest = jnp.maximum(earlier[0], later[0])
    return (
        largest,
        earlier[1] * jnp.exp(earlier[0] - largest) + later[1] * jnp.exp(later[0] - largest),
    )


def attend_in_place(queries, new_keys, new_values, cache_codes, cache_scales, lengths, place):
    rows_local = queries.shape[0]
    whole_queries, whole_keys, whole_values = (
        lax.all_gather(queries, "mp", axis=2, tiled=True),
        *sent_together((new_keys, new_values), "mp", 2, 0),
    )
    pair = whole_keys.shape[2] // KVH
    whole_keys = whole_keys.reshape(rows_local, NEW, KVH, pair, HEAD)[:, :, :, 0]
    whole_values = whole_values.reshape(rows_local, NEW, KVH, pair, HEAD)[:, :, :, 0]
    grouped = whole_queries.reshape(rows_local, NEW, KVH, QH // KVH, HEAD)
    span = cache_codes.shape[1]
    widened = cache_codes.astype(jnp.float32).reshape(
        rows_local, span // FACTOR_GROUP, FACTOR_GROUP, 2, KVH * HEAD
    )
    block_scales = cache_scales.astype(jnp.float32).reshape(
        rows_local, span // FACTOR_GROUP, 1, 2, KVH * HEAD
    )
    cache = (widened * block_scales).astype(jnp.bfloat16).reshape(rows_local, span, 2, KVH, HEAD)
    factor = HEAD ** (-0.5)
    older = (
        jnp.einsum("rtkgd,rskd->rkgts", grouped, cache[:, :, 0], preferred_element_type=jnp.float32)
        * factor
    )
    fresh = (
        jnp.einsum("rtkgd,rukd->rkgtu", grouped, whole_keys, preferred_element_type=jnp.float32)
        * factor
    )
    slots = place * span + jnp.arange(span, dtype=jnp.int32)
    older_allowed = (slots[None, :] < lengths[:, None])[:, None, None, None, :]
    steps = jnp.arange(NEW, dtype=jnp.int32)
    fresh_allowed = (steps[None, :] <= steps[:, None]) & (place == 0)
    older = jnp.where(older_allowed, older, -jnp.inf)
    fresh = jnp.where(fresh_allowed, fresh, -jnp.inf)
    top = jnp.maximum(jnp.maximum(jnp.max(older, axis=-1), jnp.max(fresh, axis=-1)), LOWEST)[
        ..., None
    ]
    total = jnp.sum(jnp.exp(older - top), axis=-1, keepdims=True) + jnp.sum(
        jnp.exp(fresh - top), axis=-1, keepdims=True
    )
    largest, whole_total = joined_all((top, total), "mp", combine_totals)
    older_weights = (jnp.exp(older - largest) / whole_total).astype(jnp.bfloat16)
    fresh_weights = (jnp.exp(fresh - largest) / whole_total).astype(jnp.bfloat16)
    partial_value = jnp.einsum(
        "rkgts,rskd->rtkgd", older_weights, cache[:, :, 1], preferred_element_type=jnp.float32
    )
    partial_value = partial_value + jnp.einsum(
        "rkgtu,rukd->rtkgd", fresh_weights, whole_values, preferred_element_type=jnp.float32
    )
    partial_value = partial_value.reshape(rows_local, NEW, QH, HEAD)
    summed = sent_and_summed(partial_value, "mp", 2)
    return summed.astype(jnp.bfloat16)


def on_device(
    token_ids,
    prompt_lengths,
    cache_codes,
    cache_scales,
    embedding,
    norm_gain,
    query_weight,
    key_value_weight,
    output_weight,
):
    parts = lax.axis_size("mp")
    place = lax.axis_index("mp")
    batch_index = lax.axis_index("dp")
    pair = max(parts // KVH, 1)
    per_device = max(KVH // parts, 1)
    rows_local = cache_codes.shape[0]
    vocab_local = embedding.shape[0]
    local_heads = query_weight.shape[1] // HEAD
    local_ids = token_ids.reshape(-1) - place * vocab_local
    inside = (local_ids >= 0) & (local_ids < vocab_local)
    picked = jnp.take(embedding, jnp.clip(local_ids, 0, vocab_local - 1), axis=0)
    embedded = tensor_total(jnp.where(inside[:, None], picked.astype(jnp.float32), 0.0))
    scaled = (embedded * norm_gain.astype(jnp.float32)).astype(jnp.bfloat16)
    squares = jnp.sum(embedded * embedded, axis=1)
    first_head = place // pair * per_device
    weight_slice = lax.dynamic_slice_in_dim(
        key_value_weight, first_head * HEAD, per_device * HEAD, axis=2
    )
    weight_slice = weight_slice.reshape(weight_slice.shape[0], 2 * per_device * HEAD)
    query_part = jnp.dot(scaled, query_weight, preferred_element_type=jnp.float32)
    fresh_part = jnp.dot(scaled, weight_slice, preferred_element_type=jnp.float32)
    query_sum, fresh_sum, square_sum = sent_together_2(
        (query_part, fresh_part, squares), "dp", 0, 1
    )
    inverse = lax.rsqrt(square_sum / D + EPSILON)[:, None]
    lengths = lax.dynamic_slice_in_dim(prompt_lengths, batch_index * rows_local, rows_local)
    positions = (lengths[:, None] + jnp.arange(NEW, dtype=jnp.int32)[None, :])[:, :, None]
    queries = rotate(
        (query_sum * inverse).reshape(rows_local, NEW, local_heads, HEAD), positions
    ).astype(jnp.bfloat16)
    fresh = (fresh_sum * inverse).reshape(rows_local, NEW, 2, per_device, HEAD)
    new_keys = rotate(fresh[:, :, 0], positions).astype(jnp.bfloat16)
    new_values = fresh[:, :, 1].astype(jnp.bfloat16)
    mixed = attend_in_place(
        queries, new_keys, new_values, cache_codes, cache_scales, lengths, place
    )
    mixed = mixed.reshape(rows_local * NEW, local_heads * HEAD)
    partial_value = jnp.dot(
        gather_directly(mixed, "dp", 0), output_weight, preferred_element_type=jnp.float32
    )
    result = tensor_total(partial_value).astype(jnp.bfloat16)
    return result.reshape(token_ids.shape[0], token_ids.shape[1], output_weight.shape[1])


def solution(mesh):
    return jax.shard_map(
        on_device,
        mesh=mesh,
        in_specs=(
            P(),
            P(),
            P("dp", "mp", None, None),
            P("dp", "mp", None, None),
            P("mp", "dp"),
            P("dp"),
            P("dp", "mp"),
            P("dp", None, None),
            P("mp", "dp"),
        ),
        out_specs=P(None, None, "dp"),
        check_vma=False,
    )
```

profile of v0, /device:TPU:2, one launch (start us, length us, event | category | flops | bytes accessed | tf_op | source)
XLA Modules:
  0.0 366.9 jit_solution(13847323160019481383)
XLA Ops:
  6.5 0.9 subtract_clamp_fusion
  7.4 0.1 copy.117
  7.5 0.1 min.18
  7.6 0.7 compare_and_fusion.1
  8.4 0.1 copy.116
  8.4 0.1 and.32
  8.5 4.7 %gather_fusion = bf16[512,512]{1,0:T(8,128)(2,1)S(1)} fusion(bf16[4032,512]{1,0:T(8,128)(2,1)} %param.13, s32[1024]{0:T(1024)S(1)} %pad_clamp_fusion), kind=kCustom, calls=%fused_computation | custom fusion | bytes 1050624 | tf_op jit(solution)/shard_map/jit(_take)/gather | solution.py:208
  13.2 0.2 convert_select_fusion
  13.5 38.3 %all_to_all.35 = f32[16,32,512]{2,1,0:T(8,128)S(1)} all-to-all(f32[16,32,512]{2,1,0:T(8,128)S(1)} %convert_select_fusion), channel_id=1, replica_groups=mesh['dp'=16,'mp'=16] {'mp'}, dimensions={0} | all-to-all | bytes 2097152 | tf_op jit(solution)/shard_map/all_to_all | solution.py:25
  51.9 1.1 broadcast_in_dim.74
  53.0 4.6 %all-to-all-start.1 = ((f32[16,32,512]{2,1,0:T(8,128)}), f32[16,32,512]{2,1,0:T(8,128)S(1)}, u32[]{:S(2)}, u32[]{:S(2)}) async-start(f32[16,32,512]{2,1,0:T(8,128)} %broadcast_in_dim.74), calls=%async_computation.1 | async-start | bytes 2097152 | tf_op jit(solution)/shard_map/all_to_all | solution.py:42
  57.7 0.2 constant_dynamic-slice_fusion
  57.9 27.4 %all-to-all-done.1 = f32[16,32,512]{2,1,0:T(8,128)S(1)} async-done(((f32[16,32,512]{2,1,0:T(8,128)}), f32[16,32,512]{2,1,0:T(8,128)S(1)}, u32[]{:S(2)}, u32[]{:S(2)}) %all-to-all-start.1) | async-done | bytes 1048608 | tf_op jit(solution)/shard_map/all_to_all | solution.py:42
  85.3 0.2 multiply_convert_fusion
  85.5 0.1 reshape.289
  85.6 0.3 fusion.17
  85.9 0.1 fusion.12
  86.1 0.5 fusion.35
  86.6 0.1 pad_maximum_fusion
  86.7 1.7 copy.140
  88.4 0.8 mul.192
  89.2 4.2 %copy.151 = f32[192,8,8,128]{3,2,1,0:T(8,128)} copy(f32[192,8,8,128]{3,1,2,0:T(8,128)S(1)} %bitcast.116) | data formatting | bytes 12582912
  93.4 8.8 %copy.112 = bf16[2,384,2,1024]{1,3,2,0:T(8,128)(2,1)} copy(bf16[2,384,2,1024]{3,2,1,0:T(2,128)(2,1)} %param.11) | data formatting | bytes 6291456 | tf_op args[2]
  102.2 5.4 %copy.114 = f32[2,384,2,8,128]{4,1,3,0,2:T(8,128)} copy(bf16[2,384,2,8,128]{1,4,3,2,0:T(8,128)(2,1)} %bitcast.118) | data formatting | bytes 9437184 | tf_op jit(solution)/shard_map/reshape | solution.py:145
  107.6 0.1 dynamic_slice.6
  107.8 0.1 broadcast_compare_fusion
  107.9 0.1 multiply_cosine_fusion.1
  108.0 7.9 %fusion = bf16[2,384,2,8,128]{4,1,3,0,2:T(8,128)(2,1)} fusion(f32[2,384,2,8,128]{4,1,3,0,2:T(8,128)} %copy.114, f32[2,384,2,8,128]{4,3,1,2,0:T(8,128)} %bitcast.117), kind=kLoop, calls=%fused_computation.2 | loop fusion | flops 3145728 | bytes 15728640 | tf_op jit(solution)/shard_map/convert_element_type | solution.py:151
  115.9 33.1 %reduce-scatter.4.cloned.1.call-done = f32[32,769]{1,0:T(8,128)} async-done(((f32[512,769]{1,0:T(8,128)}), f32[32,769]{1,0:T(8,128)}) %reduce-scatter.4.cloned.1.call-update) | async-done | bytes 98448 | tf_op jit(solution)/shard_map/reduce_scatter | solution.py:100
  149.0 0.7 add_rsqrt_fusion
  149.7 0.1 copy.154
  149.8 0.8 slice_multiply_fusion.3
  150.7 0.1 fusion.27
  150.9 0.1 pad_maximum_fusion.2
  150.9 42.0 %all_gather.7 = bf16[4,16,16,128]{3,1,0,2:T(8,128)(2,1)S(1)} all-gather(bf16[4,16,1,128]{3,1,0,2:T(8,128)(2,1)S(1)} %pad_maximum_fusion.2), channel_id=1, replica_groups=mesh['dp'=16,'mp'=16] {'mp'}, dimensions={2}, use_global_device_ids=true | all-gather | bytes 278528 | tf_op jit(solution)/shard_map/all_gather | solution.py:62
  192.9 0.9 slice_multiply_fusion.2
  193.9 0.1 subtract_convert_fusion
  194.0 0.1 pad_maximum_fusion.1
  194.1 38.7 %all_gather.6 = bf16[2,16,64,128]{3,1,0,2:T(8,128)(2,1)S(1)} all-gather(bf16[2,16,4,128]{3,1,0,2:T(8,128)(2,1)S(1)} %copy.120), channel_id=1, replica_groups=mesh['dp'=16,'mp'=16] {'mp'}, dimensions={2}, use_global_device_ids=true | all-gather | bytes 557056 | tf_op jit(solution)/shard_map/all_gather | solution.py:137
  232.8 1.4 fusion.34
  234.2 2.5 bitcast_reduce_fusion
  236.7 0.1 max.54
  236.8 0.3 exponential_reduce_fusion
  237.1 2.8 fusion.2
  240.0 0.1 add.114
  240.1 0.9 broadcast_in_dim.78
  241.0 4.3 %all-to-all-start.2 = ((f32[16,4096,1]{1,2,0:T(1,128)}), f32[16,4096,1]{1,2,0:T(1,128)S(1)}, u32[]{:S(2)}, u32[]{:S(2)}) async-start(f32[16,4096,1]{1,2,0:T(1,128)} %broadcast_in_dim.78), calls=%async_computation.2 | async-start | bytes 524288 | tf_op jit(solution)/shard_map/all_to_all | solution.py:42
  245.3 11.1 %all-to-all-done.2 = f32[16,4096,1]{1,2,0:T(1,128)S(1)} async-done(((f32[16,4096,1]{1,2,0:T(1,128)}), f32[16,4096,1]{1,2,0:T(1,128)S(1)}, u32[]{:S(2)}, u32[]{:S(2)}) %all-to-all-start.2) | async-done | bytes 262176 | tf_op jit(solution)/shard_map/all_to_all | solution.py:42
  256.5 0.7 slice_reduce_fusion
  257.1 0.4 reshape_reshape.9
  257.5 0.4 reshape_reshape.10
  257.9 0.2 multiply_add_fusion
  258.1 0.1 multiply_add_fusion.1
  258.3 1.5 copy-done.2
  259.8 2.2 fusion.7
  262.0 0.4 convolution_add_fusion
  262.4 0.1 copy.165
  262.5 24.7 %all_to_all.36 = f32[16,2,16,4,128]{4,2,3,1,0:T(8,128)S(1)} all-to-all(f32[16,2,16,4,128]{4,2,3,1,0:T(8,128)S(1)} %bitcast.121), channel_id=1, replica_groups=mesh['dp'=16,'mp'=16] {'mp'}, dimensions={0} | all-to-all | bytes 2097152 | tf_op jit(solution)/shard_map/all_to_all | solution.py:25
  287.3 17.1 %all_to_all.37 = bf16[16,32,512]{2,1,0:T(8,128)(2,1)S(1)} all-to-all(bf16[16,32,512]{2,1,0:T(8,128)(2,1)S(1)} %broadcast_in_dim.79), channel_id=1, replica_groups=mesh['dp'=16,'mp'=16] {'dp'}, dimensions={0} | all-to-all | bytes 1048576 | tf_op jit(solution)/shard_map/all_to_all | solution.py:42
  304.5 0.4 fusion.13
  304.9 32.5 %all_to_all.38 = f32[16,32,512]{2,1,0:T(8,128)S(1)} all-to-all(f32[16,32,512]{2,1,0:T(8,128)S(1)} %fusion.13), channel_id=1, replica_groups=mesh['dp'=16,'mp'=16] {'mp'}, dimensions={0} | all-to-all | bytes 2097152 | tf_op jit(solution)/shard_map/all_to_all | solution.py:25
  337.4 0.1 reduce_sum.59
  337.5 21.8 %all_to_all.39 = bf16[16,32,512]{2,1,0:T(8,128)(2,1)S(1)} all-to-all(bf16[16,32,512]{2,1,0:T(8,128)(2,1)S(1)} %broadcast_in_dim.80), channel_id=1, replica_groups=mesh['dp'=16,'mp'=16] {'mp'}, dimensions={0} | all-to-all | bytes 1048576 | tf_op jit(solution)/shard_map/all_to_all | solution.py:42
  359.3 0.8 copy.169
  (50 shorter events, 0.8 us)
Async XLA Ops:
  6.5 51.1 %copy-start = (bf16[512,2,1024]{2,1,0:T(2,128)(2,1)S(1)}, bf16[512,2,1024]{2,1,0:T(2,128)(2,1)}, u32[]{:S(2)}) copy-start(bf16[512,2,1024]{2,1,0:T(2,128)(2,1)} %param.16) | copy-start | bytes 6291460
  13.4 44.2 %copy-start.7 = (bf16[512]{0:T(512)(128)(2,1)S(1)}, bf16[512]{0:T(512)(128)(2,1)}, u32[]{:S(2)}) copy-start(bf16[512]{0:T(512)(128)(2,1)} %param.14) | copy-start | bytes 3076
  53.0 32.3 %all-to-all-start.1 = ((f32[16,32,512]{2,1,0:T(8,128)}), f32[16,32,512]{2,1,0:T(8,128)S(1)}, u32[]{:S(2)}, u32[]{:S(2)}) async-start(f32[16,32,512]{2,1,0:T(8,128)} %broadcast_in_dim.74), calls=%async_computation.1 | async-start | bytes 2097152 | tf_op jit(solution)/shard_map/all_to_all | solution.py:42
  57.6 91.4 %reduce-scatter.4.cloned.1.call-start = ((), (), s32[]{:S(2)}) async-start(), calls=%async_computation.8 | async-start | bytes 1949696 | tf_op jit(solution)/shard_map/reduce_scatter | solution.py:100
  57.9 28.2 %copy-start.4 = (bf16[512,512]{1,0:T(8,128)(2,1)S(1)}, bf16[512,512]{1,0:T(8,128)(2,1)}, u32[]{:S(2)}) copy-start(bf16[512,512]{1,0:T(8,128)(2,1)} %param.15) | copy-start | bytes 1572868
  86.7 1.7 copy-start.6
  102.2 5.4 %copy-start.8 = (s32[32]{0:T(128)S(1)}, s32[32]{0:T(128)}, u32[]{:S(2)}) copy-start(s32[32]{0:T(128)} %param.10) | copy-start | bytes 388
  193.9 40.3 %copy-start.3 = (bf16[2,384,2,8,128]{4,1,3,0,2:T(8,128)(2,1)S(1)}, bf16[2,384,2,8,128]{4,1,3,0,2:T(8,128)(2,1)}, u32[]{:S(2)}) copy-start(bf16[2,384,2,8,128]{4,1,3,0,2:T(8,128)(2,1)} %fusion) | copy-start | bytes 9437188
  241.0 15.5 %all-to-all-start.2 = ((f32[16,4096,1]{1,2,0:T(1,128)}), f32[16,4096,1]{1,2,0:T(1,128)S(1)}, u32[]{:S(2)}, u32[]{:S(2)}) async-start(f32[16,4096,1]{1,2,0:T(1,128)} %broadcast_in_dim.78), calls=%async_computation.2 | async-start | bytes 524288 | tf_op jit(solution)/shard_map/all_to_all | solution.py:42
  257.9 1.9 copy-start.2
  262.4 42.0 %copy-start.5 = (bf16[512,512]{1,0:T(8,128)(2,1)S(1)}, bf16[512,512]{1,0:T(8,128)(2,1)}, u32[]{:S(2)}) copy-start(bf16[512,512]{1,0:T(8,128)(2,1)} %param.17) | copy-start | bytes 1572868
  304.5 55.6 %copy-start.1 = (bf16[512,2,1024]{2,1,0:T(2,128)(2,1)S(1)}, bf16[512,2,1024]{2,1,0:T(2,128)(2,1)}, u32[]{:S(2)}) copy-start(bf16[512,2,1024]{2,1,0:T(2,128)(2,1)} %param.16) | copy-start | bytes 6291460
Sparse Core Ops, SparseCore 0:
  88.5 60.4 reduce-scatter.3
where the time goes:
time: 368 us; the launch traced here: 367 us
  blocking collectives  215 us (58%)
  waiting for transfers between devices  71.7 us (19%)
  local copies, waits for them, and re-layouts  32.6 us (9%)
  other arithmetic  17.1 us (5%)
  between operations  13.9 us (4%)
  starting transfers between devices  8.95 us (2%)
  matrix products  7.7 us (2%)
    all_to_all x3, blocking collectives, sent_and_summed(): lax.all_to_all(pieces, axis, split_axis=0, concat_axis=0, tiled=True)  95.5 us
    all_gather x1, blocking collectives, sent_together(): lax.all_gather(both, axis, axis=dim, tiled=True)  42 us
    all_to_all x2, blocking collectives, copy_for_each(): return lax.all_to_all(copies, axis, split_axis=0, concat_axis=0, tiled=True)  38.9 us
    all_gather x1, blocking collectives, attend_in_place(): lax.all_gather(queries, 'mp', axis=2, tiled=True)  38.7 us
    all_to_all x2, waiting for transfers between devices, copy_for_each(): return lax.all_to_all(copies, axis, split_axis=0, concat_axis=0, tiled=True)  38.6 us
    reduce_scatter x1, waiting for transfers between devices, sent_together_2(): whole = lax.psum_scatter(both, axis, scatter_dimension=dim, tiled=True)  33.1 us
    unnamed x27, local copies, waits for them, and re-layouts  17.1 us
    all_to_all x2, starting transfers between devices, copy_for_each(): return lax.all_to_all(copies, axis, split_axis=0, concat_axis=0, tiled=True)  8.9 us
  transfers between devices with their start and end apart: 3, of which 3 were waited for; matrix products, arithmetic and copies ran while one was open for 8% of the time, Pallas kernels for 0%

commit v1 on v0

--- a/solution.py
+++ b/solution.py
@@ -13,6 +13,13 @@
 ROPE_BASE = 500000.0
 EPSILON = 1e-05
 LOWEST = -1e30
+
+
+def swapped_in(x, mesh_axis, d):
+    size = lax.axis_size(mesh_axis)
+    parts = jnp.stack([x for _ in range(size)])
+    parts = lax.all_to_all(parts, mesh_axis, split_axis=0, concat_axis=0)
+    return jnp.concatenate(parts, axis=d)
 
 
 def split_up(shard, dim, devices):
@@ -134,7 +141,7 @@
 def attend_in_place(queries, new_keys, new_values, cache_codes, cache_scales, lengths, place):
     rows_local = queries.shape[0]
     whole_queries, whole_keys, whole_values = (
-        lax.all_gather(queries, "mp", axis=2, tiled=True),
+        swapped_in(queries, "mp", 2),
         *sent_together((new_keys, new_values), "mp", 2, 0),
     )
     pair = whole_keys.shape[2] // KVH

time: 368 us -> 344 us (0.935)
  blocking collectives: 215 us -> 182 us
  starting transfers between devices: 8.95 us -> 16.8 us
    all_gather x1 -> x0, blocking collectives: 38.7 us -> none  [attend_in_place(): lax.all_gather(queries, 'mp', axis=2, tiled=True)]
    all_to_all x0 -> x1, starting transfers between devices: none -> 8.6 us  [swapped_in(): parts = lax.all_to_all(parts, mesh_axis, split_axis=0, concat_axis=0)]
    all_to_all x2, blocking collectives: 38.9 us -> 43.1 us  [copy_for_each(): return lax.all_to_all(copies, axis, split_axis=0, concat_axis=0, tiled=True)]
    unnamed x27 -> x25, local copies, waits for them, and re-layouts: 17.1 us -> 17.1 us
  transfers between devices with their start and end apart: 3 -> 4, of which waited for: 3 -> 3; matrix products, arithmetic and copies ran while one was open for 8% -> 8% of each run, Pallas kernels for 0% -> 0%
where the time goes in v1:
time: 344 us; the launch traced here: 343 us
  blocking collectives  182 us (53%)
  waiting for transfers between devices  70.9 us (21%)
  local copies, waits for them, and re-layouts  33.5 us (10%)
  other arithmetic  17.1 us (5%)
  starting transfers between devices  16.8 us (5%)
  between operations  13.9 us (4%)
  matrix products  9.09 us (3%)
    all_to_all x3, blocking collectives, sent_and_summed(): lax.all_to_all(pieces, axis, split_axis=0, concat_axis=0, tiled=True)  95 us
    all_gather x1, blocking collectives, sent_together(): lax.all_gather(both, axis, axis=dim, tiled=True)  43.6 us
    all_to_all x2, blocking collectives, copy_for_each(): return lax.all_to_all(copies, axis, split_axis=0, concat_axis=0, tiled=True)  43.1 us
    all_to_all x2, waiting for transfers between devices, copy_for_each(): return lax.all_to_all(copies, axis, split_axis=0, concat_axis=0, tiled=True)  37.8 us
    reduce_scatter x1, waiting for transfers between devices, sent_together_2(): whole = lax.psum_scatter(both, axis, scatter_dimension=dim, tiled=True)  33.1 us
    unnamed x25, local copies, waits for them, and re-layouts  17.1 us
    all_to_all x1, starting transfers between devices, swapped_in(): parts = lax.all_to_all(parts, mesh_axis, split_axis=0, concat_axis=0)  8.6 us
    all_to_all x2, starting transfers between devices, copy_for_each(): return lax.all_to_all(copies, axis, split_axis=0, concat_axis=0, tiled=True)  8.11 us
  transfers between devices with their start and end apart: 4, of which 3 were waited for; matrix products, arithmetic and copies ran while one was open for 8% of the time, Pallas kernels for 0%

profile of v1, /device:TPU:2, one launch (start us, length us, event | category | flops | bytes accessed | tf_op | source)
XLA Modules:
  0.0 342.9 jit_solution(2878115428056862522)
XLA Ops:
  6.5 0.9 subtract_clamp_fusion
  7.4 0.1 copy.117
  7.5 0.1 min.18
  7.6 0.7 compare_and_fusion.1
  8.4 0.1 copy.116
  8.4 0.1 and.32
  8.5 4.7 %gather_fusion = bf16[512,512]{1,0:T(8,128)(2,1)S(1)} fusion(bf16[4032,512]{1,0:T(8,128)(2,1)} %param.13, s32[1024]{0:T(1024)S(1)} %pad_clamp_fusion), kind=kCustom, calls=%fused_computation | custom fusion | bytes 1050624 | tf_op jit(solution)/shard_map/jit(_take)/gather | solution.py:215
  13.2 0.2 convert_select_fusion
  13.5 38.3 %all_to_all.40 = f32[16,32,512]{2,1,0:T(8,128)S(1)} all-to-all(f32[16,32,512]{2,1,0:T(8,128)S(1)} %convert_select_fusion), channel_id=1, replica_groups=mesh['dp'=16,'mp'=16] {'mp'}, dimensions={0} | all-to-all | bytes 2097152 | tf_op jit(solution)/shard_map/all_to_all | solution.py:32
  51.9 1.1 broadcast_in_dim.74
  53.0 4.6 %all-to-all-start.1 = ((f32[16,32,512]{2,1,0:T(8,128)}), f32[16,32,512]{2,1,0:T(8,128)S(1)}, u32[]{:S(2)}, u32[]{:S(2)}) async-start(f32[16,32,512]{2,1,0:T(8,128)} %broadcast_in_dim.74), calls=%async_computation.1 | async-start | bytes 2097152 | tf_op jit(solution)/shard_map/all_to_all | solution.py:49
  57.7 0.2 constant_dynamic-slice_fusion
  57.9 27.4 %all-to-all-done.1 = f32[16,32,512]{2,1,0:T(8,128)S(1)} async-done(((f32[16,32,512]{2,1,0:T(8,128)}), f32[16,32,512]{2,1,0:T(8,128)S(1)}, u32[]{:S(2)}, u32[]{:S(2)}) %all-to-all-start.1) | async-done | bytes 1048608 | tf_op jit(solution)/shard_map/all_to_all | solution.py:49
  85.3 0.2 multiply_convert_fusion
  85.5 0.1 reshape.296
  85.6 0.3 fusion.19
  85.9 0.1 fusion.12
  86.1 0.5 fusion.37
  86.6 0.1 pad_maximum_fusion
  86.7 1.7 copy.140
  88.4 0.8 mul.192
  89.2 4.2 %copy.151 = f32[192,8,8,128]{3,2,1,0:T(8,128)} copy(f32[192,8,8,128]{3,1,2,0:T(8,128)S(1)} %bitcast.127) | data formatting | bytes 12582912
  93.4 8.8 %copy.112 = bf16[2,384,2,1024]{1,3,2,0:T(8,128)(2,1)} copy(bf16[2,384,2,1024]{3,2,1,0:T(2,128)(2,1)} %param.11) | data formatting | bytes 6291456 | tf_op args[2]
  102.2 5.4 %copy.114 = f32[2,384,2,8,128]{4,1,3,0,2:T(8,128)} copy(bf16[2,384,2,8,128]{1,4,3,2,0:T(8,128)(2,1)} %bitcast.129) | data formatting | bytes 9437184 | tf_op jit(solution)/shard_map/reshape | solution.py:152
  107.6 0.1 dynamic_slice.6
  107.8 0.1 multiply_cosine_fusion.1
  108.0 7.9 %fusion = bf16[2,384,2,8,128]{4,1,3,0,2:T(8,128)(2,1)} fusion(f32[2,384,2,8,128]{4,1,3,0,2:T(8,128)} %copy.114, f32[2,384,2,8,128]{4,3,1,2,0:T(8,128)} %bitcast.128), kind=kLoop, calls=%fused_computation.2 | loop fusion | flops 3145728 | bytes 15728640 | tf_op jit(solution)/shard_map/convert_element_type | solution.py:158
  115.9 33.1 %reduce-scatter.4.cloned.1.call-done = f32[32,769]{1,0:T(8,128)} async-done(((f32[512,769]{1,0:T(8,128)}), f32[32,769]{1,0:T(8,128)}) %reduce-scatter.4.cloned.1.call-update) | async-done | bytes 98448 | tf_op jit(solution)/shard_map/reduce_scatter | solution.py:107
  149.0 0.7 add_rsqrt_fusion
  149.7 0.1 copy.154
  149.8 0.9 slice_multiply_fusion.2
  150.7 0.1 subtract_convert_fusion
  150.8 0.1 pad_maximum_fusion.1
  151.0 0.9 stack.2
  151.9 8.6 %all-to-all-start.2 = ((bf16[16,2,16,4,128]{4,2,3,1,0:T(8,128)(2,1)}), bf16[16,2,16,4,128]{4,2,3,1,0:T(8,128)(2,1)S(1)}, u32[]{:S(2)}, u32[]{:S(2)}) async-start(bf16[16,2,16,4,128]{4,2,3,1,0:T(8,128)(2,1)} %stack.2), calls=%async_computation.2 | async-start | bytes 1048576 | tf_op jit(solution)/shard_map/all_to_all | solution.py:21
  160.5 0.8 slice_multiply_fusion.3
  161.4 0.1 fusion.29
  161.6 0.1 pad_maximum_fusion.2
  161.6 43.6 %all_gather.3 = bf16[4,16,16,128]{3,1,0,2:T(8,128)(2,1)S(1)} all-gather(bf16[4,16,1,128]{3,1,0,2:T(8,128)(2,1)S(1)} %pad_maximum_fusion.2), channel_id=1, replica_groups=mesh['dp'=16,'mp'=16] {'mp'}, dimensions={2}, use_global_device_ids=true | all-gather | bytes 278528 | tf_op jit(solution)/shard_map/all_gather | solution.py:69
  205.3 1.4 fusion.36
  206.7 3.9 %bitcast_reduce_fusion = (f32[2,8,8,16]{3,2,1,0:T(8,128)S(1)}, f32[2,8,384,16,8]{2,3,4,1,0:T(8,128)}) fusion(pred[2,384]{1,0:T(4,128)(4,1)S(1)} %broadcast_compare_fusion, bf16[2,384,2,8,128]{4,1,3,0,2:T(8,128)(2,1)} %fusion, bf16[2,16,8,8,128]{4,1,3,2,0:T(8,128)(2,1)S(1)} %bitcast.131), kind=kOutput, calls=%fused_computation.5 | convolution fusion | flops 203683840 | bytes 5251840 | tf_op jit(solution)/shard_map/rtkgd,rskd->rkgts/dot_general | solution.py:161
  210.5 0.1 max.54
  210.6 0.3 exponential_reduce_fusion
  210.9 2.8 fusion.2
  213.8 0.1 add.114
  213.9 0.9 broadcast_in_dim.78
  214.8 3.5 %all-to-all-start.3 = ((f32[16,4096,1]{1,2,0:T(1,128)}), f32[16,4096,1]{1,2,0:T(1,128)S(1)}, u32[]{:S(2)}, u32[]{:S(2)}) async-start(f32[16,4096,1]{1,2,0:T(1,128)} %broadcast_in_dim.78), calls=%async_computation.3 | async-start | bytes 524288 | tf_op jit(solution)/shard_map/all_to_all | solution.py:49
  218.4 10.4 %all-to-all-done.3 = f32[16,4096,1]{1,2,0:T(1,128)S(1)} async-done(((f32[16,4096,1]{1,2,0:T(1,128)}), f32[16,4096,1]{1,2,0:T(1,128)S(1)}, u32[]{:S(2)}, u32[]{:S(2)}) %all-to-all-start.3) | async-done | bytes 262176 | tf_op jit(solution)/shard_map/all_to_all | solution.py:49
  228.8 0.7 slice_reduce_fusion
  229.4 0.4 reshape_reshape.13
  229.8 0.4 reshape_reshape.14
  230.2 0.2 multiply_add_fusion
  230.4 0.1 multiply_add_fusion.1
  230.6 1.5 copy-done.2
  232.0 2.2 fusion.7
  234.3 0.4 convolution_add_fusion
  234.7 0.1 copy.165
  234.8 23.6 %all_to_all.41 = f32[16,2,16,4,128]{4,2,3,1,0:T(8,128)S(1)} all-to-all(f32[16,2,16,4,128]{4,2,3,1,0:T(8,128)S(1)} %bitcast.134), channel_id=1, replica_groups=mesh['dp'=16,'mp'=16] {'mp'}, dimensions={0} | all-to-all | bytes 2097152 | tf_op jit(solution)/shard_map/all_to_all | solution.py:32
  258.6 21.3 %all_to_all.42 = bf16[16,32,512]{2,1,0:T(8,128)(2,1)S(1)} all-to-all(bf16[16,32,512]{2,1,0:T(8,128)(2,1)S(1)} %broadcast_in_dim.79), channel_id=1, replica_groups=mesh['dp'=16,'mp'=16] {'dp'}, dimensions={0} | all-to-all | bytes 1048576 | tf_op jit(solution)/shard_map/all_to_all | solution.py:49
  279.9 0.4 fusion.13
  280.3 33.0 %all_to_all.43 = f32[16,32,512]{2,1,0:T(8,128)S(1)} all-to-all(f32[16,32,512]{2,1,0:T(8,128)S(1)} %fusion.13), channel_id=1, replica_groups=mesh['dp'=16,'mp'=16] {'mp'}, dimensions={0} | all-to-all | bytes 2097152 | tf_op jit(solution)/shard_map/all_to_all | solution.py:32
  313.3 0.1 reduce_sum.59
  313.5 21.8 %all_to_all.44 = bf16[16,32,512]{2,1,0:T(8,128)(2,1)S(1)} all-to-all(bf16[16,32,512]{2,1,0:T(8,128)(2,1)S(1)} %broadcast_in_dim.80), channel_id=1, replica_groups=mesh['dp'=16,'mp'=16] {'mp'}, dimensions={0} | all-to-all | bytes 1048576 | tf_op jit(solution)/shard_map/all_to_all | solution.py:49
  335.3 0.8 copy.169
  (50 shorter events, 0.9 us)
Async XLA Ops:
  6.5 51.1 %copy-start = (bf16[512,2,1024]{2,1,0:T(2,128)(2,1)S(1)}, bf16[512,2,1024]{2,1,0:T(2,128)(2,1)}, u32[]{:S(2)}) copy-start(bf16[512,2,1024]{2,1,0:T(2,128)(2,1)} %param.16) | copy-start | bytes 6291460
  13.4 44.2 %copy-start.6 = (bf16[512]{0:T(512)(128)(2,1)S(1)}, bf16[512]{0:T(512)(128)(2,1)}, u32[]{:S(2)}) copy-start(bf16[512]{0:T(512)(128)(2,1)} %param.14) | copy-start | bytes 3076
  53.0 32.3 %all-to-all-start.1 = ((f32[16,32,512]{2,1,0:T(8,128)}), f32[16,32,512]{2,1,0:T(8,128)S(1)}, u32[]{:S(2)}, u32[]{:S(2)}) async-start(f32[16,32,512]{2,1,0:T(8,128)} %broadcast_in_dim.74), calls=%async_computation.1 | async-start | bytes 2097152 | tf_op jit(solution)/shard_map/all_to_all | solution.py:49
  57.6 91.4 %reduce-scatter.4.cloned.1.call-start = ((), (), s32[]{:S(2)}) async-start(), calls=%async_computation.9 | async-start | bytes 1949696 | tf_op jit(solution)/shard_map/reduce_scatter | solution.py:107
  57.9 28.2 %copy-start.3 = (bf16[512,512]{1,0:T(8,128)(2,1)S(1)}, bf16[512,512]{1,0:T(8,128)(2,1)}, u32[]{:S(2)}) copy-start(bf16[512,512]{1,0:T(8,128)(2,1)} %param.15) | copy-start | bytes 1572868
  86.7 1.7 copy-start.5
  102.2 5.4 %copy-start.7 = (s32[32]{0:T(128)S(1)}, s32[32]{0:T(128)}, u32[]{:S(2)}) copy-start(s32[32]{0:T(128)} %param.10) | copy-start | bytes 388
  151.9 53.4 %all-to-all-start.2 = ((bf16[16,2,16,4,128]{4,2,3,1,0:T(8,128)(2,1)}), bf16[16,2,16,4,128]{4,2,3,1,0:T(8,128)(2,1)S(1)}, u32[]{:S(2)}, u32[]{:S(2)}) async-start(bf16[16,2,16,4,128]{4,2,3,1,0:T(8,128)(2,1)} %stack.2), calls=%async_computation.2 | async-start | bytes 1048576 | tf_op jit(solution)/shard_map/all_to_all | solution.py:21
  214.8 13.9 %all-to-all-start.3 = ((f32[16,4096,1]{1,2,0:T(1,128)}), f32[16,4096,1]{1,2,0:T(1,128)S(1)}, u32[]{:S(2)}, u32[]{:S(2)}) async-start(f32[16,4096,1]{1,2,0:T(1,128)} %broadcast_in_dim.78), calls=%async_computation.3 | async-start | bytes 524288 | tf_op jit(solution)/shard_map/all_to_all | solution.py:49
  230.1 1.9 copy-start.2
  234.7 45.2 %copy-start.4 = (bf16[512,512]{1,0:T(8,128)(2,1)S(1)}, bf16[512,512]{1,0:T(8,128)(2,1)}, u32[]{:S(2)}) copy-start(bf16[512,512]{1,0:T(8,128)(2,1)} %param.17) | copy-start | bytes 1572868
  279.9 56.2 %copy-start.1 = (bf16[512,2,1024]{2,1,0:T(2,128)(2,1)S(1)}, bf16[512,2,1024]{2,1,0:T(2,128)(2,1)}, u32[]{:S(2)}) copy-start(bf16[512,2,1024]{2,1,0:T(2,128)(2,1)} %param.16) | copy-start | bytes 6291460
Sparse Core Ops, SparseCore 0:
  88.5 60.4 reduce-scatter.3
